TPU v7x, 32 devices: a whole 2x2x4 slice. The times are simulated.
32 devices in a mesh: rows: 8 (over y, x, core), rep: 4 (over z).
Axes of the slice: x: 2, y: 2, z: 4, core: 2. Of those that a mesh axis runs over, the one named last changes fastest.
Arguments:
- x_tiles: bfloat16 [64, 10, 128, 128], P('rows'), may hold values from -2.5 to 2.5
- giant_tiles: bfloat16 [64, 10, 128, 128], P('rows'), may hold values from -2.5 to 2.5
- coeffs: float32 [3], replicated, may hold values from 0.5 to 1.5
- pattern: int32 [64, 10], replicated, may hold values from 0 to 63, as said below
Outputs:
- squared: bfloat16 [64, 10, 128, 128], P('rows')
- result: bfloat16 [64, 10, 128, 128], P('rows')
Inputs may be any that keep to these rules, and one draw needn't show every extreme that they name: `pattern`: slots 2 j and 2 j + 1 of block row i hold two different tile columns of panel (i // 8 + j - 2) mod (8), a panel being 8 consecutive block rows, for j = 0 to 4; slot 4 holds i itself.
All inputs are finite; a program needn't handle non-finite values.
Results may differ from a plain program's by a relative error of at most 0.012.
Values may be sent and summed in bfloat16 or wider, within the bound.
No kernel may reach another device: no remote copies, remote signals or barrier semaphores. Data moves between devices by JAX's collectives and lax.ppermute only.
A program may use at most 128 MiB of HBM per device.

v0:
```python
import functools

import jax
import jax.numpy as jnp
from jax import lax
from jax.experimental import pallas as pl
from jax.experimental.pallas import tpu as pltpu
from jax.sharding import PartitionSpec as P


HALF = 2
KP = 2
CLASSES = 2 * HALF

COST = 2**20
VMEM_LIMIT = 16 * 2**20


def down_offset(panel, kind):
    return (kind - panel + HALF) % CLASSES - HALF


def classes_of(rep):
    return (rep % 2, rep % 2 + 2)


def route(panels, reps, target, kept=lambda panel, rep: True):
    pairs = []
    for rep in range(reps):
        for panel in range(panels):
            to_panel, to_rep = target(panel, rep)
            to_panel %= panels
            if kept(to_panel, to_rep):
                pairs.append((panel * reps + rep, to_panel * reps + to_rep))
    return pairs


def permute(block, pairs):
    return lax.ppermute(block, ("rows", "rep"), pairs)


def table_kernel(pattern, table, *, blocks):
    count = pattern.shape[1]
    device = lax.axis_index("rows")

    def one_row(i, carry):
        mine = [pattern[device * blocks + i, u] for u in range(count)]
        for s in range(count):
            theirs = [pattern[mine[s], t] for t in range(count)]
            place = lax.rem(mine[s], blocks) * KP
            for u in range(count):
                offset = u // KP - s // KP
                found = jnp.int32(-1)
                if abs(offset) <= HALF:
                    for e in range(KP):
                        same = theirs[(offset + HALF) * KP + e] == mine[u]
                        found = jnp.where(same, place + e, found)
                table[(i * count + s) * count + u] = found
        return carry

    lax.fori_loop(0, blocks, one_row, 0)


def here(chunk, swapped=False):
    device, rep = lax.axis_index("rows"), lax.axis_index("rep")
    parity = lax.rem(rep + 1 if swapped else rep, 2)
    return down_offset(device, parity + 2 * chunk), lax.rem(device, 2) == 0


def row_product(left, regions, table, i, slot, begin, end):
    count = left.shape[1]

    def met(s, e):
        where = table[(i * count + s) * count + slot + e]
        tile = regions[s // KP][jnp.maximum(where, 0)]
        return jnp.where(where >= 0, tile, jnp.zeros_like(tile))

    lefts = jnp.concatenate([left[i, s] for s in range(begin, end)], axis=1)
    rights = jnp.concatenate(
        [jnp.concatenate([met(s, e) for e in range(KP)], axis=1) for s in range(begin, end)], axis=0
    )
    return jnp.dot(lefts, rights, preferred_element_type=jnp.float32)


def regions_of(parity, offset, own0, own1, core, near, two, forwarded):
    own = own0 if (offset == HALF) == (parity == 0) else own1
    if parity == 0:
        return (two, near, own, core, forwarded)
    return (forwarded, core, own, near, two)


def bounds_of(offset):
    return max(0, offset) * KP, (2 * HALF + 1 + min(0, offset)) * KP


def branches(chunk, run):
    mine, even = here(chunk)
    for parity in range(2):
        for offset in range(-HALF, HALF):

            @pl.when(jnp.logical_and(mine == offset, even == (parity == 0)))
            def _(parity=parity, offset=offset):
                run(parity, offset)


def halves(total):
    rounded = total.astype(jnp.bfloat16)
    tile = total.shape[0]
    return [rounded[:, e * tile : (e + 1) * tile] for e in range(KP)]


def first_kernel(chunk, table, coeffs, left, *refs):
    sources, (main, extra, send0, send1) = refs[:6], refs[6:]
    blocks, tile = left.shape[0], left.shape[2]

    def one_unit(parity, offset, sums, sends):
        slot = (offset + HALF) * KP
        regions = regions_of(parity, offset, *sources)

        def one_row(i, carry):
            total = row_product(left, regions, table, i, slot, *bounds_of(offset))
            for e, part in enumerate(halves(total)):
                sums[i, e] = part
                mixed = coeffs[1] * left[i, slot + e].astype(jnp.float32) + coeffs[2] * part.astype(
                    jnp.float32
                )
                if slot + e == HALF * KP:
                    line = lax.broadcasted_iota(jnp.int32, (tile, tile), 0)
                    column = lax.broadcasted_iota(jnp.int32, (tile, tile), 1)
                    mixed = jnp.where(line == column, coeffs[0], 0.0) + mixed
                for send in sends:
                    send[i, e] = mixed.astype(jnp.bfloat16)
            return carry

        lax.fori_loop(0, blocks, one_row, 0)

    def run(parity, offset):
        if offset > -HALF:
            one_unit(parity, offset, main, (send0, send1))
        else:
            one_unit(parity, -HALF, main, (send1 if parity == 0 else send0,))
            one_unit(parity, HALF, extra, (send0 if parity == 0 else send1,))

    branches(chunk, run)


def early_kernel(chunk, table, left, own0, own1, core, near, forwarded, extra, partial):
    blocks, count = left.shape[0], left.shape[1]

    def regions(parity, offset):
        return regions_of(parity, offset, own0, own1, core, near, None, forwarded)

    def whole_unit(parity, offset):
        def one_row(i, carry):
            total = row_product(
                left, regions(parity, offset), table, i, (offset + HALF) * KP, *bounds_of(offset)
            )
            for e, part in enumerate(halves(total)):
                extra[i, e] = part
            return carry

        lax.fori_loop(0, blocks, one_row, 0)

    def part_unit(parity, offset):
        begin, end = bounds_of(offset)
        begin, end = (max(begin, KP), end) if parity == 0 else (begin, min(end, count - KP))

        def one_row(i, carry):
            partial[i] = row_product(
                left, regions(parity, offset), table, i, (offset + HALF) * KP, begin, end
            )
            return carry

        lax.fori_loop(0, blocks, one_row, 0)

    def run(parity, offset):
        if offset > -HALF:
            part_unit(parity, offset)
        else:
            sign = 1 if parity == 0 else -1
            whole_unit(parity, sign * HALF)
            part_unit(parity, -sign * HALF)

    branches(chunk, run)


def late_kernel(chunk, table, left, two, partial, main):
    blocks, count = left.shape[0], left.shape[1]
    offset, even = here(chunk)
    odd = jnp.logical_not(even)
    slot = jnp.where(jnp.logical_and(offset == -HALF, odd), 2 * HALF, offset + HALF) * KP

    def rows(begin):
        def one_row(i, carry):
            total = partial[i] + row_product(
                left, (two,) * count, table, i, slot, begin, begin + KP
            )
            for e, part in enumerate(halves(total)):
                main[i, e] = part
            return carry

        lax.fori_loop(0, blocks, one_row, 0)

    pl.when(odd)(lambda: rows(count - KP))
    pl.when(jnp.logical_not(odd))(lambda: rows(0))


def call(kernel, operands, outs, scratch=(), full_at=None):
    arrays, specs = [], []
    for space, array in operands:
        specs.append(pl.BlockSpec(memory_space=space))
        if space in (pltpu.VMEM, pltpu.HBM):
            array = pltpu.with_memory_space_constraint(array, space)
        arrays.append(array)
    return pl.pallas_call(
        kernel,
        out_shape=[space(out.shape, out.dtype) for space, out in outs],
        in_specs=specs,
        out_specs=[pl.BlockSpec(memory_space=space) for space, _ in outs],
        scratch_shapes=scratch,
        input_output_aliases={} if full_at is None else {full_at: 0},
        compiler_params=pltpu.CompilerParams(vmem_limit_bytes=VMEM_LIMIT),
        cost_estimate=pl.CostEstimate(flops=COST, bytes_accessed=2**23, transcendentals=0),
    )(*arrays)


def units_of(tiles):
    blocks, tile = tiles.shape[0], tiles.shape[2]
    return pltpu.VMEM, jax.ShapeDtypeStruct((blocks, KP, tile, tile), tiles.dtype)


def flat(block):
    return pltpu.VMEM, block.reshape((-1,) + block.shape[2:])


def first_product(chunk, table, coeffs, left, rights):
    operands = [(pltpu.SMEM, table), (pltpu.SMEM, coeffs), (pltpu.VMEM, left)]
    return call(
        functools.partial(first_kernel, chunk),
        operands + [flat(r) for r in rights],
        [units_of(left)] * 4,
    )


def early_product(chunk, table, left, rights):
    rights = rights[:4] + rights[5:]
    blocks, tile = left.shape[0], left.shape[2]
    partial = jax.ShapeDtypeStruct((blocks, tile, KP * tile), jnp.float32)
    return call(
        functools.partial(early_kernel, chunk),
        [(pltpu.SMEM, table), (pltpu.VMEM, left)] + [flat(r) for r in rights],
        [units_of(left), (pltpu.VMEM, partial)],
    )


def late_product(chunk, table, left, two, partial):
    return call(
        functools.partial(late_kernel, chunk),
        [(pltpu.SMEM, table), (pltpu.VMEM, left), flat(two), (pltpu.VMEM, partial)],
        [units_of(left)],
    )[0]


def place_kernel(names, aliased, *refs):
    parts, full, sems = refs[aliased : aliased + len(names)], refs[-2], refs[-1]
    slots, counts = [], []
    for chunk, swapped, second, mirrored in names:
        offset, even = here(chunk, swapped)
        both = offset == -HALF
        low = (offset + HALF) * KP
        high = 2 * HALF * KP
        turned = jnp.logical_and(both, jnp.logical_not(even))
        if second:
            slots.append(jnp.where(even, high, 0) if mirrored else high)
            counts.append(both)
        else:
            slots.append(jnp.where(turned, high, low) if mirrored else low)
            counts.append(None)

    def store(k):
        target = full.at[:, pl.ds(slots[k], KP)]
        return pltpu.make_async_copy(parts[k], target, sems.at[k])

    for step in (lambda k: store(k).start(), lambda k: store(k).wait()):
        for k, count in enumerate(counts):
            if count is None:
                step(k)
            else:
                pl.when(count)(functools.partial(step, k))


def place(shape, full, parts):
    names = tuple(name for name, _ in parts)
    units = [(pltpu.VMEM, unit) for _, unit in parts]
    aliased = 0 if full is None else 1
    return call(
        functools.partial(place_kernel, names, aliased),
        [(pltpu.HBM, full)] * aliased + units,
        [(pltpu.HBM, shape)],
        [pltpu.SemaphoreType.DMA((len(parts),))],
        0 if aliased else None,
    )[0]


def pick_kernel(chunk, tiles, out0, out1, sems):
    down, even = here(chunk)
    up = jnp.where(down == -HALF, HALF, down)
    offsets = (jnp.where(even, up, down), jnp.where(even, down, up))
    loads = [
        pltpu.make_async_copy(tiles.at[:, pl.ds((offsets[k] + HALF) * KP, KP)], out, sems.at[k])
        for k, out in enumerate((out0, out1))
    ]
    for load in loads:
        load.start()
    for load in loads:
        load.wait()


def pick(chunk, tiles):
    return call(
        functools.partial(pick_kernel, chunk),
        [(pltpu.HBM, tiles)],
        [units_of(tiles)] * 2,
        [pltpu.SemaphoreType.DMA((2,))],
    )


def tile_table(pattern, blocks):
    size = blocks * pattern.shape[1] ** 2
    return call(
        functools.partial(table_kernel, blocks=blocks),
        [(pltpu.SMEM, pattern)],
        [(pltpu.SMEM, jax.ShapeDtypeStruct((size,), jnp.int32))],
    )[0]


def local(x_tiles, giant_tiles, coeffs, pattern):
    blocks = x_tiles.shape[0]
    panels = lax.axis_size("rows")
    reps = lax.axis_size("rep")

    def swapped(panel):
        return panel + 1 if panel % 2 == 0 else panel - 1

    core_route = route(panels, reps, lambda p, z: (swapped(p), z))
    near_route = route(panels, reps, lambda p, z: (p - 1 if p % 2 == 0 else p + 1, z))

    def two_route(chunk):
        return route(
            panels,
            reps,
            lambda p, z: (p + 2 if p % 2 == 0 else p - 2, z),
            lambda p, z: (classes_of(z)[chunk] - p) % CLASSES != (1 if p % 2 == 0 else 3),
        )

    partner_route = route(panels, reps, lambda p, z: (p, z ^ 1))

    def extra_route(chunk):
        return route(
            panels,
            reps,
            lambda p, z: (p, z ^ 1),
            lambda p, z: down_offset(p, classes_of(z ^ 1)[chunk]) == -HALF,
        )

    def gathered(chunk, send0, send1):
        near = permute(send1, near_route)
        two = permute(send0, two_route(chunk))
        core = permute(send0, core_route)
        forwarded = permute(near, core_route)
        return (send0, send1, core, near, two, forwarded)

    def swapped_parts(chunk, main, extra):
        main = permute(main, partner_route)
        extra = permute(extra, extra_route(chunk))
        return main, extra

    rights = []
    for chunk in range(2):
        send0, send1 = pick(chunk, x_tiles)
        rights.append(gathered(chunk, send0, send1))
    table = tile_table(pattern, blocks)
    shape = jax.ShapeDtypeStruct(x_tiles.shape, x_tiles.dtype)

    babies = []
    parts = []
    for chunk in range(2):
        main, extra, send0, send1 = first_product(
            chunk, table, coeffs, x_tiles, rights[chunk]
        )
        babies.append(gathered(chunk, send0, send1))
        parts += [((chunk, False, False, False), main), ((chunk, False, True, False), extra)]
        main, extra = swapped_parts(chunk, main, extra)
        parts += [((chunk, True, False, False), main), ((chunk, True, True, False), extra)]
    squared = place(shape, None, parts)

    parts = []
    for chunk in range(2):
        extra, partial = early_product(chunk, table, giant_tiles, babies[chunk])
        main = late_product(chunk, table, giant_tiles, babies[chunk][4], partial)
        parts += [((chunk, False, True, True), extra), ((chunk, False, False, True), main)]
        main, extra = swapped_parts(chunk, main, extra)
        parts += [((chunk, True, True, True), extra), ((chunk, True, False, True), main)]
    result = place(shape, None, parts[:-1])
    result = place(shape, result, parts[-1:])
    return (squared, result)


def solution(mesh):
    return jax.shard_map(
        local,
        mesh=mesh,
        in_specs=(P("rows", None, None, None), P("rows", None, None, None), P(), P()),
        out_specs=(P("rows", None, None, None), P("rows", None, None, None)),
        check_vma=False,
    )
```

profile of v0, /device:TPU:1, one launch (start us, length us, event | category | flops | bytes accessed | tf_op | source)
XLA Modules:
  0.0 137.4 jit_solution(3628500713441533195)
XLA Ops:
  0.7 2.2 %shard_map.60 = (bf16[8,2,128,128]{3,2,1,0:T(8,128)(2,1)}, bf16[8,2,128,128]{3,2,1,0:T(8,128)(2,1)S(1)}) custom-call(bf16[8,10,128,128]{3,2,1,0:T(8,128)(2,1)} %left.7), custom_call_target="tpu_custom_call" | custom-call | flops 1048576 | bytes 8388608 | tf_op jit(solution)/shard_map/pallas_call | solution.py:215
  2.9 2.7 %collective-permute-start.1 = (bf16[8,2,128,128]{3,2,1,0:T(8,128)(2,1)S(1)}, bf16[8,2,128,128]{3,2,1,0:T(8,128)(2,1)}, u32[]{:S(2)}, u32[]{:S(2)}) collective-permute-start(bf16[8,2,128,128]{3,2,1,0:T(8,128)(2,1)S(1)} %get-tuple-element.19), channel_id=1, source_target_pairs={{0,28},{4,8},{8,4},{12,16},{16,12},{20,24},{24,20},{28,0},{1,29},{... | collective-permute-start | bytes 1572872 | tf_op jit(solution)/shard_map/ppermute | solution.py:39
  9.2 4.1 %collective-permute-start.2 = (bf16[8,2,128,128]{3,2,1,0:T(8,128)(2,1)}, bf16[8,2,128,128]{3,2,1,0:T(8,128)(2,1)}, u32[]{:S(2)}, u32[]{:S(2)}) collective-permute-start(bf16[8,2,128,128]{3,2,1,0:T(8,128)(2,1)} %get-tuple-element.18), channel_id=1, source_target_pairs={{0,8},{4,28},{8,16},{16,24},{20,12},{24,0},{1,9},{5,29},{13,5},{17... | collective-permute-start | bytes 1572872 | tf_op jit(solution)/shard_map/ppermute | solution.py:39
  13.3 4.1 %collective-permute-done.1 = bf16[8,2,128,128]{3,2,1,0:T(8,128)(2,1)} collective-permute-done((bf16[8,2,128,128]{3,2,1,0:T(8,128)(2,1)S(1)}, bf16[8,2,128,128]{3,2,1,0:T(8,128)(2,1)}, u32[]{:S(2)}, u32[]{:S(2)}) %collective-permute-start.1) | collective-permute-done | bytes 524320 | tf_op jit(solution)/shard_map/ppermute | solution.py:39
  19.4 1.3 collective-permute-start.8
  20.7 8.0 %collective-permute-done.7 = bf16[8,2,128,128]{3,2,1,0:T(8,128)(2,1)} collective-permute-done((bf16[8,2,128,128]{3,2,1,0:T(8,128)(2,1)S(1)}, bf16[8,2,128,128]{3,2,1,0:T(8,128)(2,1)}, u32[]{:S(2)}, u32[]{:S(2)}) %collective-permute-start.7) | collective-permute-done | bytes 524320 | tf_op jit(solution)/shard_map/ppermute | solution.py:39
  30.0 3.1 %shard_map.59.table = s32[800]{0:T(1024)S(4)} custom-call(s32[64,10]{1,0:T(8,128)S(1)} %copy.7.pattern), custom_call_target="tpu_custom_call" | custom-call | flops 1048576 | bytes 8388608 | tf_op jit(solution)/shard_map/pallas_call | solution.py:215
  33.0 5.8 %collective-permute-done.2 = bf16[8,2,128,128]{3,2,1,0:T(8,128)(2,1)} collective-permute-done((bf16[8,2,128,128]{3,2,1,0:T(8,128)(2,1)}, bf16[8,2,128,128]{3,2,1,0:T(8,128)(2,1)}, u32[]{:S(2)}, u32[]{:S(2)}) %collective-permute-start.2) | collective-permute-done | bytes 524320 | tf_op jit(solution)/shard_map/ppermute | solution.py:39
  41.0 3.9 %shard_map.61 = (bf16[8,2,128,128]{3,2,1,0:T(8,128)(2,1)S(1)}, bf16[8,2,128,128]{3,2,1,0:T(8,128)(2,1)S(1)}, bf16[8,2,128,128]{3,2,1,0:T(8,128)(2,1)S(1)}, bf16[8,2,128,128]{3,2,1,0:T(8,128)(2,1)S(1)}) custom-call(s32[800]{0:T(1024)S(4)} %shard_map.59.table, f32[3]{0:T(128)S(1)} %copy-done.8, bf16[8,10,128,128]{3,2,1,0:T(8,128)(2,1)S(1)} %copy-done, ...), custom_call_target="tpu_custom_call" | custom-call | flops 1048576 | bytes 8388608 | tf_op jit(solution)/shard_map/pallas_call | solution.py:215
  44.8 5.2 %collective-permute-start.13 = (bf16[8,2,128,128]{3,2,1,0:T(8,128)(2,1)S(1)}, bf16[8,2,128,128]{3,2,1,0:T(8,128)(2,1)S(1)}, u32[]{:S(2)}, u32[]{:S(2)}) collective-permute-start(bf16[8,2,128,128]{3,2,1,0:T(8,128)(2,1)S(1)} %get-tuple-element.27), channel_id=1, source_target_pairs={{0,28},{4,8},{8,4},{12,16},{16,12},{20,24},{24,20},{28,0},{1,29},{... | collective-permute-start | bytes 1572872 | tf_op jit(solution)/shard_map/ppermute | solution.py:39
  50.1 4.0 %shard_map.63 = (bf16[8,2,128,128]{3,2,1,0:T(8,128)(2,1)S(1)}, bf16[8,2,128,128]{3,2,1,0:T(8,128)(2,1)S(1)}, bf16[8,2,128,128]{3,2,1,0:T(8,128)(2,1)S(1)}, bf16[8,2,128,128]{3,2,1,0:T(8,128)(2,1)S(1)}) custom-call(s32[800]{0:T(1024)S(4)} %shard_map.59.table, f32[3]{0:T(128)S(1)} %copy-done.8, bf16[8,10,128,128]{3,2,1,0:T(8,128)(2,1)S(1)} %copy-done, ...), custom_call_target="tpu_custom_call" | custom-call | flops 1048576 | bytes 8388608 | tf_op jit(solution)/shard_map/pallas_call | solution.py:215
  54.4 4.4 %collective-permute-start.15 = (bf16[8,2,128,128]{3,2,1,0:T(8,128)(2,1)S(1)}, bf16[8,2,128,128]{3,2,1,0:T(8,128)(2,1)S(1)}, u32[]{:S(2)}, u32[]{:S(2)}) collective-permute-start(bf16[8,2,128,128]{3,2,1,0:T(8,128)(2,1)S(1)} %get-tuple-element.26), channel_id=1, source_target_pairs={{0,8},{4,28},{8,16},{16,24},{20,12},{24,0},{1,9},{5,29},{13,5},{17... | collective-permute-start | bytes 1572872 | tf_op jit(solution)/shard_map/ppermute | solution.py:39
  59.9 2.9 %collective-permute-done.13 = bf16[8,2,128,128]{3,2,1,0:T(8,128)(2,1)S(1)} collective-permute-done((bf16[8,2,128,128]{3,2,1,0:T(8,128)(2,1)S(1)}, bf16[8,2,128,128]{3,2,1,0:T(8,128)(2,1)S(1)}, u32[]{:S(2)}, u32[]{:S(2)}) %collective-permute-start.13) | collective-permute-done | bytes 524320 | tf_op jit(solution)/shard_map/ppermute | solution.py:39
  62.8 10.2 %collective-permute-done.19 = bf16[8,2,128,128]{3,2,1,0:T(8,128)(2,1)S(1)} collective-permute-done((bf16[8,2,128,128]{3,2,1,0:T(8,128)(2,1)S(1)}, bf16[8,2,128,128]{3,2,1,0:T(8,128)(2,1)S(1)}, u32[]{:S(2)}, u32[]{:S(2)}) %collective-permute-start.19) | collective-permute-done | bytes 524320 | tf_op jit(solution)/shard_map/ppermute | solution.py:39
  73.0 1.7 %collective-permute-start.4 = (bf16[8,2,128,128]{3,2,1,0:T(8,128)(2,1)S(1)}, bf16[8,2,128,128]{3,2,1,0:T(8,128)(2,1)S(1)}, u32[]{:S(2)}, u32[]{:S(2)}) collective-permute-start(bf16[8,2,128,128]{3,2,1,0:T(8,128)(2,1)S(1)} %get-tuple-element.20.refs_0_), channel_id=1, source_target_pairs={{0,1},{4,5},{8,9},{12,13},{16,17},{20,21},{24,25},{28,29},{1,0},{5... | collective-permute-start | bytes 1572872 | tf_op jit(solution)/shard_map/ppermute | solution.py:39
  74.7 7.8 %collective-permute-done.15 = bf16[8,2,128,128]{3,2,1,0:T(8,128)(2,1)S(1)} collective-permute-done((bf16[8,2,128,128]{3,2,1,0:T(8,128)(2,1)S(1)}, bf16[8,2,128,128]{3,2,1,0:T(8,128)(2,1)S(1)}, u32[]{:S(2)}, u32[]{:S(2)}) %collective-permute-start.15) | collective-permute-done | bytes 524320 | tf_op jit(solution)/shard_map/ppermute | solution.py:39
  83.2 1.3 collective-permute-start.21
  84.5 6.2 %collective-permute-start.10 = (bf16[8,2,128,128]{3,2,1,0:T(8,128)(2,1)S(1)}, bf16[8,2,128,128]{3,2,1,0:T(8,128)(2,1)S(1)}, u32[]{:S(2)}, u32[]{:S(2)}) collective-permute-start(bf16[8,2,128,128]{3,2,1,0:T(8,128)(2,1)S(1)} %get-tuple-element.24.refs_4_), channel_id=1, source_target_pairs={{0,1},{4,5},{8,9},{12,13},{16,17},{20,21},{24,25},{28,29},{1,0},{5... | collective-permute-start | bytes 1572872 | tf_op jit(solution)/shard_map/ppermute | solution.py:39
  90.7 2.2 %shard_map.65 = (bf16[8,2,128,128]{3,2,1,0:T(8,128)(2,1)S(1)}, f32[8,128,256]{2,1,0:T(8,128)S(1)}) custom-call(s32[800]{0:T(1024)S(4)} %shard_map.59.table, bf16[8,10,128,128]{3,2,1,0:T(8,128)(2,1)S(1)} %copy-done.1, bf16[16,128,128]{2,1,0:T(8,128)(2,1)S(1)} %bitcast.25, bf16[16,128,128]{2,1,0:T(8,128)(2,1)S(1)} %bitcast.26, ...), custom_call_target="tpu_custom_call" | custom-call | flops 1048576 | bytes 8388608 | tf_op jit(solution)/shard_map/pallas_call | solution.py:215
  92.9 1.4 %shard_map.66.refs_1_ = bf16[8,2,128,128]{3,2,1,0:T(8,128)(2,1)S(1)} custom-call(s32[800]{0:T(1024)S(4)} %shard_map.59.table, bf16[8,10,128,128]{3,2,1,0:T(8,128)(2,1)S(1)} %copy-done.1, bf16[16,128,128]{2,1,0:T(8,128)(2,1)S(1)} %bitcast.38, f32[8,128,256]{2,1,0:T(8,128)S(1)} %get-tuple-element.29.partial), custom_call_target="tpu_custom_call" | custom-call | flops 1048576 | bytes 8388608 | tf_op jit(solution)/shard_map/pallas_call | solution.py:215
  94.4 1.3 collective-permute-start.11
  95.7 2.0 %shard_map.67 = (bf16[8,2,128,128]{3,2,1,0:T(8,128)(2,1)S(1)}, f32[8,128,256]{2,1,0:T(8,128)S(1)}) custom-call(s32[800]{0:T(1024)S(4)} %shard_map.59.table, bf16[8,10,128,128]{3,2,1,0:T(8,128)(2,1)S(1)} %copy-done.1, bf16[16,128,128]{2,1,0:T(8,128)(2,1)S(1)} %bitcast.24, bf16[16,128,128]{2,1,0:T(8,128)(2,1)S(1)} %bitcast.27, ...), custom_call_target="tpu_custom_call" | custom-call | flops 1048576 | bytes 8388608 | tf_op jit(solution)/shard_map/pallas_call | solution.py:215
  98.4 3.8 %collective-permute-start.17 = (bf16[8,2,128,128]{3,2,1,0:T(8,128)(2,1)S(1)}, bf16[8,2,128,128]{3,2,1,0:T(8,128)(2,1)S(1)}, u32[]{:S(2)}, u32[]{:S(2)}) collective-permute-start(bf16[8,2,128,128]{3,2,1,0:T(8,128)(2,1)S(1)} %shard_map.66.refs_1_), channel_id=1, source_target_pairs={{0,1},{4,5},{8,9},{12,13},{16,17},{20,21},{24,25},{28,29},{1,0},{5... | collective-permute-start | bytes 1572872 | tf_op jit(solution)/shard_map/ppermute | solution.py:39
  102.2 1.3 collective-permute-start.22
  103.5 1.4 %shard_map.68.refs_5_ = bf16[8,2,128,128]{3,2,1,0:T(8,128)(2,1)S(1)} custom-call(s32[800]{0:T(1024)S(4)} %shard_map.59.table, bf16[8,10,128,128]{3,2,1,0:T(8,128)(2,1)S(1)} %copy-done.1, bf16[16,128,128]{2,1,0:T(8,128)(2,1)S(1)} %bitcast.37, f32[8,128,256]{2,1,0:T(8,128)S(1)} %get-tuple-element.33.partial), custom_call_target="tpu_custom_call" | custom-call | flops 1048576 | bytes 8388608 | tf_op jit(solution)/shard_map/pallas_call | solution.py:215
  105.0 2.2 %collective-permute-start.23 = (bf16[8,2,128,128]{3,2,1,0:T(8,128)(2,1)S(1)}, bf16[8,2,128,128]{3,2,1,0:T(8,128)(2,1)S(1)}, u32[]{:S(2)}, u32[]{:S(2)}) collective-permute-start(bf16[8,2,128,128]{3,2,1,0:T(8,128)(2,1)S(1)} %shard_map.68.refs_5_), channel_id=1, source_target_pairs={{0,1},{4,5},{8,9},{12,13},{16,17},{20,21},{24,25},{28,29},{1,0},{5... | collective-permute-start | bytes 1572872 | tf_op jit(solution)/shard_map/ppermute | solution.py:39
  107.1 3.2 %collective-permute-done.11.refs_7_ = bf16[8,2,128,128]{3,2,1,0:T(8,128)(2,1)S(1)} collective-permute-done((bf16[8,2,128,128]{3,2,1,0:T(8,128)(2,1)S(1)}, bf16[8,2,128,128]{3,2,1,0:T(8,128)(2,1)S(1)}, u32[]{:S(2)}, u32[]{:S(2)}) %collective-permute-start.11) | collective-permute-done | bytes 524320 | tf_op jit(solution)/shard_map/ppermute | solution.py:39
  110.4 1.6 %shard_map.64 = bf16[8,10,128,128]{3,2,1,0:T(8,128)(2,1)} custom-call(bf16[8,2,128,128]{3,2,1,0:T(8,128)(2,1)S(1)} %get-tuple-element.20.refs_0_, bf16[8,2,128,128]{3,2,1,0:T(8,128)(2,1)S(1)} %get-tuple-element.21.refs_1_, bf16[8,2,128,128]{3,2,1,0:T(8,128)(2,1)S(1)} %collective-permute-done.4.refs_2_, ...), custom_call_target="tpu_custom_call" | custom-call | flops 1048576 | bytes 8388608 | tf_op jit(solution)/shard_map/pallas_call | solution.py:215
  112.0 9.7 %collective-permute-done.17.refs_3_ = bf16[8,2,128,128]{3,2,1,0:T(8,128)(2,1)S(1)} collective-permute-done((bf16[8,2,128,128]{3,2,1,0:T(8,128)(2,1)S(1)}, bf16[8,2,128,128]{3,2,1,0:T(8,128)(2,1)S(1)}, u32[]{:S(2)}, u32[]{:S(2)}) %collective-permute-start.17) | collective-permute-done | bytes 524320 | tf_op jit(solution)/shard_map/ppermute | solution.py:39
  121.6 9.4 %collective-permute-done.22.refs_6_ = bf16[8,2,128,128]{3,2,1,0:T(8,128)(2,1)S(1)} collective-permute-done((bf16[8,2,128,128]{3,2,1,0:T(8,128)(2,1)S(1)}, bf16[8,2,128,128]{3,2,1,0:T(8,128)(2,1)S(1)}, u32[]{:S(2)}, u32[]{:S(2)}) %collective-permute-start.22) | collective-permute-done | bytes 524320 | tf_op jit(solution)/shard_map/ppermute | solution.py:39
  131.0 1.4 shard_map.69.refs_0_
  132.4 4.2 %collective-permute-done.23.refs_1_ = bf16[8,2,128,128]{3,2,1,0:T(8,128)(2,1)S(1)} collective-permute-done((bf16[8,2,128,128]{3,2,1,0:T(8,128)(2,1)S(1)}, bf16[8,2,128,128]{3,2,1,0:T(8,128)(2,1)S(1)}, u32[]{:S(2)}, u32[]{:S(2)}) %collective-permute-start.23) | collective-permute-done | bytes 524320 | tf_op jit(solution)/shard_map/ppermute | solution.py:39
  (49 shorter events, 12.6 us)
Async XLA Ops:
  0.6 38.2 %copy-start = (bf16[8,10,128,128]{3,2,1,0:T(8,128)(2,1)S(1)}, bf16[8,10,128,128]{3,2,1,0:T(8,128)(2,1)}, u32[]{:S(2)}) copy-start(bf16[8,10,128,128]{3,2,1,0:T(8,128)(2,1)} %left.7) | copy-start | bytes 7864324
  0.6 29.2 %copy-start.9 = (s32[64,10]{0,1:T(8,128)S(1)}, s32[64,10]{0,1:T(8,128)}, u32[]{:S(2)}) copy-start(s32[64,10]{0,1:T(8,128)} %param.7) | copy-start | bytes 7684
  0.7 38.2 %copy-start.8 = (f32[3]{0:T(128)S(1)}, f32[3]{0:T(128)}, u32[]{:S(2)}) copy-start(f32[3]{0:T(128)} %coeffs.3) | copy-start | bytes 40
  2.8 25.9 %copy-start.4 = (bf16[8,2,128,128]{3,2,1,0:T(8,128)(2,1)}, bf16[8,2,128,128]{3,2,1,0:T(8,128)(2,1)S(1)}, u32[]{:S(2)}) copy-start(bf16[8,2,128,128]{3,2,1,0:T(8,128)(2,1)S(1)} %get-tuple-element.19) | copy-start | bytes 1572868
  2.9 14.6 %collective-permute-start.1 = (bf16[8,2,128,128]{3,2,1,0:T(8,128)(2,1)S(1)}, bf16[8,2,128,128]{3,2,1,0:T(8,128)(2,1)}, u32[]{:S(2)}, u32[]{:S(2)}) collective-permute-start(bf16[8,2,128,128]{3,2,1,0:T(8,128)(2,1)S(1)} %get-tuple-element.19), channel_id=1, source_target_pairs={{0,28},{4,8},{8,4},{12,16},{16,12},{20,24},{24,20},{28,0},{1,29},{... | collective-permute-start | bytes 1572872 | tf_op jit(solution)/shard_map/ppermute | solution.py:39
  5.5 13.1 %collective-permute-start = (bf16[8,2,128,128]{3,2,1,0:T(8,128)(2,1)}, bf16[8,2,128,128]{3,2,1,0:T(8,128)(2,1)S(1)}, u32[]{:S(2)}, u32[]{:S(2)}) collective-permute-start(bf16[8,2,128,128]{3,2,1,0:T(8,128)(2,1)} %get-tuple-element.18), channel_id=1, source_target_pairs={{0,4},{4,0},{8,12},{12,8},{16,20},{20,16},{24,28},{28,24},{1,5},{5... | collective-permute-start | bytes 1572872 | tf_op jit(solution)/shard_map/ppermute | solution.py:39
  7.5 21.2 %collective-permute-start.7 = (bf16[8,2,128,128]{3,2,1,0:T(8,128)(2,1)S(1)}, bf16[8,2,128,128]{3,2,1,0:T(8,128)(2,1)}, u32[]{:S(2)}, u32[]{:S(2)}) collective-permute-start(bf16[8,2,128,128]{3,2,1,0:T(8,128)(2,1)S(1)} %get-tuple-element.23), channel_id=1, source_target_pairs={{0,28},{4,8},{8,4},{12,16},{16,12},{20,24},{24,20},{28,0},{1,29},{... | collective-permute-start | bytes 1572872 | tf_op jit(solution)/shard_map/ppermute | solution.py:39
  9.2 29.6 %collective-permute-start.2 = (bf16[8,2,128,128]{3,2,1,0:T(8,128)(2,1)}, bf16[8,2,128,128]{3,2,1,0:T(8,128)(2,1)}, u32[]{:S(2)}, u32[]{:S(2)}) collective-permute-start(bf16[8,2,128,128]{3,2,1,0:T(8,128)(2,1)} %get-tuple-element.18), channel_id=1, source_target_pairs={{0,8},{4,28},{8,16},{16,24},{20,12},{24,0},{1,9},{5,29},{13,5},{17... | collective-permute-start | bytes 1572872 | tf_op jit(solution)/shard_map/ppermute | solution.py:39
  17.5 21.4 %collective-permute-start.3 = (bf16[8,2,128,128]{3,2,1,0:T(8,128)(2,1)}, bf16[8,2,128,128]{3,2,1,0:T(8,128)(2,1)}, u32[]{:S(2)}, u32[]{:S(2)}) collective-permute-start(bf16[8,2,128,128]{3,2,1,0:T(8,128)(2,1)} %collective-permute-done.1), channel_id=1, source_target_pairs={{0,4},{4,0},{8,12},{12,8},{16,20},{20,16},{24,28},{28,24},{1,5},{5... | collective-permute-start | bytes 1572872 | tf_op jit(solution)/shard_map/ppermute | solution.py:39
  18.6 31.4 %collective-permute-start.6 = (bf16[8,2,128,128]{3,2,1,0:T(8,128)(2,1)S(1)}, bf16[8,2,128,128]{3,2,1,0:T(8,128)(2,1)}, u32[]{:S(2)}, u32[]{:S(2)}) collective-permute-start(bf16[8,2,128,128]{3,2,1,0:T(8,128)(2,1)S(1)} %get-tuple-element.22), channel_id=1, source_target_pairs={{0,4},{4,0},{8,12},{12,8},{16,20},{20,16},{24,28},{28,24},{1,5},{5... | collective-permute-start | bytes 1572872 | tf_op jit(solution)/shard_map/ppermute | solution.py:39
  19.4 30.6 %collective-permute-start.8 = (bf16[8,2,128,128]{3,2,1,0:T(8,128)(2,1)S(1)}, bf16[8,2,128,128]{3,2,1,0:T(8,128)(2,1)}, u32[]{:S(2)}, u32[]{:S(2)}) collective-permute-start(bf16[8,2,128,128]{3,2,1,0:T(8,128)(2,1)S(1)} %get-tuple-element.22), channel_id=1, source_target_pairs={{0,8},{8,16},{12,4},{16,24},{24,0},{28,20},{5,29},{9,17},{13,5},{2... | collective-permute-start | bytes 1572872 | tf_op jit(solution)/shard_map/ppermute | solution.py:39
  28.7 21.3 %collective-permute-start.9 = (bf16[8,2,128,128]{3,2,1,0:T(8,128)(2,1)}, bf16[8,2,128,128]{3,2,1,0:T(8,128)(2,1)}, u32[]{:S(2)}, u32[]{:S(2)}) collective-permute-start(bf16[8,2,128,128]{3,2,1,0:T(8,128)(2,1)} %collective-permute-done.7), channel_id=1, source_target_pairs={{0,4},{4,0},{8,12},{12,8},{16,20},{20,16},{24,28},{28,24},{1,5},{5... | collective-permute-start | bytes 1572872 | tf_op jit(solution)/shard_map/ppermute | solution.py:39
  38.9 1.0 copy-start.5
  39.9 1.0 copy-start.7
  41.0 9.1 %copy-start.3 = (bf16[8,2,128,128]{3,2,1,0:T(8,128)(2,1)S(1)}, bf16[8,2,128,128]{3,2,1,0:T(8,128)(2,1)}, u32[]{:S(2)}) copy-start(bf16[8,2,128,128]{3,2,1,0:T(8,128)(2,1)} %copy-done.2) | copy-start | bytes 1572868
  44.8 18.0 %collective-permute-start.13 = (bf16[8,2,128,128]{3,2,1,0:T(8,128)(2,1)S(1)}, bf16[8,2,128,128]{3,2,1,0:T(8,128)(2,1)S(1)}, u32[]{:S(2)}, u32[]{:S(2)}) collective-permute-start(bf16[8,2,128,128]{3,2,1,0:T(8,128)(2,1)S(1)} %get-tuple-element.27), channel_id=1, source_target_pairs={{0,28},{4,8},{8,4},{12,16},{16,12},{20,24},{24,20},{28,0},{1,29},{... | collective-permute-start | bytes 1572872 | tf_op jit(solution)/shard_map/ppermute | solution.py:39
  50.0 40.7 %copy-start.1 = (bf16[8,10,128,128]{3,2,1,0:T(8,128)(2,1)S(1)}, bf16[8,10,128,128]{3,2,1,0:T(8,128)(2,1)}, u32[]{:S(2)}) copy-start(bf16[8,10,128,128]{3,2,1,0:T(8,128)(2,1)} %left.11) | copy-start | bytes 7864324
  54.1 18.9 %collective-permute-start.19 = (bf16[8,2,128,128]{3,2,1,0:T(8,128)(2,1)S(1)}, bf16[8,2,128,128]{3,2,1,0:T(8,128)(2,1)S(1)}, u32[]{:S(2)}, u32[]{:S(2)}) collective-permute-start(bf16[8,2,128,128]{3,2,1,0:T(8,128)(2,1)S(1)} %get-tuple-element.31), channel_id=1, source_target_pairs={{0,28},{4,8},{8,4},{12,16},{16,12},{20,24},{24,20},{28,0},{1,29},{... | collective-permute-start | bytes 1572872 | tf_op jit(solution)/shard_map/ppermute | solution.py:39
  54.4 18.6 %collective-permute-start.12 = (bf16[8,2,128,128]{3,2,1,0:T(8,128)(2,1)S(1)}, bf16[8,2,128,128]{3,2,1,0:T(8,128)(2,1)S(1)}, u32[]{:S(2)}, u32[]{:S(2)}) collective-permute-start(bf16[8,2,128,128]{3,2,1,0:T(8,128)(2,1)S(1)} %get-tuple-element.26), channel_id=1, source_target_pairs={{0,4},{4,0},{8,12},{12,8},{16,20},{20,16},{24,28},{28,24},{1,5},{5... | collective-permute-start | bytes 1572872 | tf_op jit(solution)/shard_map/ppermute | solution.py:39
  54.4 28.1 %collective-permute-start.15 = (bf16[8,2,128,128]{3,2,1,0:T(8,128)(2,1)S(1)}, bf16[8,2,128,128]{3,2,1,0:T(8,128)(2,1)S(1)}, u32[]{:S(2)}, u32[]{:S(2)}) collective-permute-start(bf16[8,2,128,128]{3,2,1,0:T(8,128)(2,1)S(1)} %get-tuple-element.26), channel_id=1, source_target_pairs={{0,8},{4,28},{8,16},{16,24},{20,12},{24,0},{1,9},{5,29},{13,5},{17... | collective-permute-start | bytes 1572872 | tf_op jit(solution)/shard_map/ppermute | solution.py:39
  58.8 24.4 %collective-permute-start.18 = (bf16[8,2,128,128]{3,2,1,0:T(8,128)(2,1)S(1)}, bf16[8,2,128,128]{3,2,1,0:T(8,128)(2,1)S(1)}, u32[]{:S(2)}, u32[]{:S(2)}) collective-permute-start(bf16[8,2,128,128]{3,2,1,0:T(8,128)(2,1)S(1)} %get-tuple-element.30), channel_id=1, source_target_pairs={{0,4},{4,0},{8,12},{12,8},{16,20},{20,16},{24,28},{28,24},{1,5},{5... | collective-permute-start | bytes 1572872 | tf_op jit(solution)/shard_map/ppermute | solution.py:39
  62.8 21.7 %collective-permute-start.14 = (bf16[8,2,128,128]{3,2,1,0:T(8,128)(2,1)S(1)}, bf16[8,2,128,128]{3,2,1,0:T(8,128)(2,1)S(1)}, u32[]{:S(2)}, u32[]{:S(2)}) collective-permute-start(bf16[8,2,128,128]{3,2,1,0:T(8,128)(2,1)S(1)} %collective-permute-done.13), channel_id=1, source_target_pairs={{0,4},{4,0},{8,12},{12,8},{16,20},{20,16},{24,28},{28,24},{1,5},{5... | collective-permute-start | bytes 1572872 | tf_op jit(solution)/shard_map/ppermute | solution.py:39
  73.0 21.4 %collective-permute-start.20 = (bf16[8,2,128,128]{3,2,1,0:T(8,128)(2,1)S(1)}, bf16[8,2,128,128]{3,2,1,0:T(8,128)(2,1)S(1)}, u32[]{:S(2)}, u32[]{:S(2)}) collective-permute-start(bf16[8,2,128,128]{3,2,1,0:T(8,128)(2,1)S(1)} %collective-permute-done.19), channel_id=1, source_target_pairs={{0,4},{4,0},{8,12},{12,8},{16,20},{20,16},{24,28},{28,24},{1,5},{5... | collective-permute-start | bytes 1572872 | tf_op jit(solution)/shard_map/ppermute | solution.py:39
  73.0 24.6 %collective-permute-start.4 = (bf16[8,2,128,128]{3,2,1,0:T(8,128)(2,1)S(1)}, bf16[8,2,128,128]{3,2,1,0:T(8,128)(2,1)S(1)}, u32[]{:S(2)}, u32[]{:S(2)}) collective-permute-start(bf16[8,2,128,128]{3,2,1,0:T(8,128)(2,1)S(1)} %get-tuple-element.20.refs_0_), channel_id=1, source_target_pairs={{0,1},{4,5},{8,9},{12,13},{16,17},{20,21},{24,25},{28,29},{1,0},{5... | collective-permute-start | bytes 1572872 | tf_op jit(solution)/shard_map/ppermute | solution.py:39
  82.5 15.9 %collective-permute-start.5 = (bf16[8,2,128,128]{3,2,1,0:T(8,128)(2,1)S(1)}, bf16[8,2,128,128]{3,2,1,0:T(8,128)(2,1)S(1)}, u32[]{:S(2)}, u32[]{:S(2)}) collective-permute-start(bf16[8,2,128,128]{3,2,1,0:T(8,128)(2,1)S(1)} %get-tuple-element.21.refs_1_), channel_id=1, source_target_pairs={{8,9},{24,25},{13,12},{29,28},{10,11},{26,27},{15,14},{31,30}} | collective-permute-start | bytes 1572872 | tf_op jit(solution)/shard_map/ppermute | solution.py:39
  83.2 19.0 %collective-permute-start.21 = (bf16[8,2,128,128]{3,2,1,0:T(8,128)(2,1)S(1)}, bf16[8,2,128,128]{3,2,1,0:T(8,128)(2,1)S(1)}, u32[]{:S(2)}, u32[]{:S(2)}) collective-permute-start(bf16[8,2,128,128]{3,2,1,0:T(8,128)(2,1)S(1)} %get-tuple-element.30), channel_id=1, source_target_pairs={{0,8},{8,16},{12,4},{16,24},{24,0},{28,20},{5,29},{9,17},{13,5},{2... | collective-permute-start | bytes 1572872 | tf_op jit(solution)/shard_map/ppermute | solution.py:39
  84.5 20.4 %collective-permute-start.10 = (bf16[8,2,128,128]{3,2,1,0:T(8,128)(2,1)S(1)}, bf16[8,2,128,128]{3,2,1,0:T(8,128)(2,1)S(1)}, u32[]{:S(2)}, u32[]{:S(2)}) collective-permute-start(bf16[8,2,128,128]{3,2,1,0:T(8,128)(2,1)S(1)} %get-tuple-element.24.refs_4_), channel_id=1, source_target_pairs={{0,1},{4,5},{8,9},{12,13},{16,17},{20,21},{24,25},{28,29},{1,0},{5... | collective-permute-start | bytes 1572872 | tf_op jit(solution)/shard_map/ppermute | solution.py:39
  94.4 16.0 %collective-permute-start.11 = (bf16[8,2,128,128]{3,2,1,0:T(8,128)(2,1)S(1)}, bf16[8,2,128,128]{3,2,1,0:T(8,128)(2,1)S(1)}, u32[]{:S(2)}, u32[]{:S(2)}) collective-permute-start(bf16[8,2,128,128]{3,2,1,0:T(8,128)(2,1)S(1)} %get-tuple-element.25.refs_5_), channel_id=1, source_target_pairs={{0,1},{16,17},{5,4},{21,20},{2,3},{18,19},{7,6},{23,22}} | collective-permute-start | bytes 1572872 | tf_op jit(solution)/shard_map/ppermute | solution.py:39
  97.7 14.3 %collective-permute-start.16 = (bf16[8,2,128,128]{3,2,1,0:T(8,128)(2,1)S(1)}, bf16[8,2,128,128]{3,2,1,0:T(8,128)(2,1)S(1)}, u32[]{:S(2)}, u32[]{:S(2)}) collective-permute-start(bf16[8,2,128,128]{3,2,1,0:T(8,128)(2,1)S(1)} %get-tuple-element.28.refs_0_), channel_id=1, source_target_pairs={{8,9},{24,25},{13,12},{29,28},{10,11},{26,27},{15,14},{31,30}} | collective-permute-start | bytes 1572872 | tf_op jit(solution)/shard_map/ppermute | solution.py:39
  98.4 23.2 %collective-permute-start.17 = (bf16[8,2,128,128]{3,2,1,0:T(8,128)(2,1)S(1)}, bf16[8,2,128,128]{3,2,1,0:T(8,128)(2,1)S(1)}, u32[]{:S(2)}, u32[]{:S(2)}) collective-permute-start(bf16[8,2,128,128]{3,2,1,0:T(8,128)(2,1)S(1)} %shard_map.66.refs_1_), channel_id=1, source_target_pairs={{0,1},{4,5},{8,9},{12,13},{16,17},{20,21},{24,25},{28,29},{1,0},{5... | collective-permute-start | bytes 1572872 | tf_op jit(solution)/shard_map/ppermute | solution.py:39
  102.2 28.8 %collective-permute-start.22 = (bf16[8,2,128,128]{3,2,1,0:T(8,128)(2,1)S(1)}, bf16[8,2,128,128]{3,2,1,0:T(8,128)(2,1)S(1)}, u32[]{:S(2)}, u32[]{:S(2)}) collective-permute-start(bf16[8,2,128,128]{3,2,1,0:T(8,128)(2,1)S(1)} %get-tuple-element.32.refs_4_), channel_id=1, source_target_pairs={{0,1},{16,17},{5,4},{21,20},{2,3},{18,19},{7,6},{23,22}} | collective-permute-start | bytes 1572872 | tf_op jit(solution)/shard_map/ppermute | solution.py:39
  105.0 31.6 %collective-permute-start.23 = (bf16[8,2,128,128]{3,2,1,0:T(8,128)(2,1)S(1)}, bf16[8,2,128,128]{3,2,1,0:T(8,128)(2,1)S(1)}, u32[]{:S(2)}, u32[]{:S(2)}) collective-permute-start(bf16[8,2,128,128]{3,2,1,0:T(8,128)(2,1)S(1)} %shard_map.68.refs_5_), channel_id=1, source_target_pairs={{0,1},{4,5},{8,9},{12,13},{16,17},{20,21},{24,25},{28,29},{1,0},{5... | collective-permute-start | bytes 1572872 | tf_op jit(solution)/shard_map/ppermute | solution.py:39
  (2 other events, 1.6 us)
where the time goes:
time: 138 us; the launch traced here: 137 us
  waiting for transfers between devices  65.5 us (47%)
  starting transfers between devices  42.1 us (31%)
  Pallas kernels  25.1 us (18%)
  local copies, waits for them, and re-layouts  3.81 us (3%)
    ppermute x24, waiting for transfers between devices, permute(): return lax.ppermute(block, ('rows', 'rep'), pairs)  65.5 us
    ppermute x24, starting transfers between devices, permute(): return lax.ppermute(block, ('rows', 'rep'), pairs)  42.1 us
    pallas_call x12, Pallas kernels, call(): pl.pallas_call(kernel, out_shape=[space(out.shape, out.dtype) for space,...  25.1 us
    unnamed x21, local copies, waits for them, and re-layouts  3.81 us
  transfers between devices with their start and end apart: 24, of which 10 were waited for; matrix products, arithmetic and copies ran while one was open for 0% of the time, Pallas kernels for 16%

commit v1 on v0

--- a/solution.py
+++ b/solution.py
@@ -39,14 +39,14 @@
     return lax.ppermute(block, ("rows", "rep"), pairs)
 
 
-def table_kernel(pattern, table, *, blocks):
-    count = pattern.shape[1]
+def table_kernel(columns, table, *, blocks):
+    count = columns.shape[0]
     device = lax.axis_index("rows")
 
     def one_row(i, carry):
-        mine = [pattern[device * blocks + i, u] for u in range(count)]
+        mine = [columns[u, device * blocks + i] for u in range(count)]
         for s in range(count):
-            theirs = [pattern[mine[s], t] for t in range(count)]
+            theirs = [columns[t, mine[s]] for t in range(count)]
             place = lax.rem(mine[s], blocks) * KP
             for u in range(count):
                 offset = u // KP - s // KP
@@ -144,42 +144,43 @@
     branches(chunk, run)
 
 
-def early_kernel(chunk, table, left, own0, own1, core, near, forwarded, extra, partial):
-    blocks, count = left.shape[0], left.shape[1]
-
-    def regions(parity, offset):
-        return regions_of(parity, offset, own0, own1, core, near, None, forwarded)
-
-    def whole_unit(parity, offset):
+def whole_kernel(chunk, table, left, own0, own1, core, forwarded, extra):
+    def run(parity, offset):
+        if offset > -HALF:
+            return
+        offset = HALF if parity == 0 else -HALF
+        regions = regions_of(parity, offset, own0, own1, core, None, None, forwarded)
+
         def one_row(i, carry):
             total = row_product(
-                left, regions(parity, offset), table, i, (offset + HALF) * KP, *bounds_of(offset)
+                left, regions, table, i, (offset + HALF) * KP, *bounds_of(offset)
             )
             for e, part in enumerate(halves(total)):
                 extra[i, e] = part
             return carry
 
-        lax.fori_loop(0, blocks, one_row, 0)
-
-    def part_unit(parity, offset):
+        lax.fori_loop(0, left.shape[0], one_row, 0)
+
+    branches(chunk, run)
+
+
+def part_kernel(chunk, table, left, own0, own1, core, near, forwarded, partial):
+    count = left.shape[1]
+
+    def run(parity, offset):
+        if offset == -HALF and parity == 1:
+            offset = HALF
+        regions = regions_of(parity, offset, own0, own1, core, near, None, forwarded)
         begin, end = bounds_of(offset)
         begin, end = (max(begin, KP), end) if parity == 0 else (begin, min(end, count - KP))
 
         def one_row(i, carry):
             partial[i] = row_product(
-                left, regions(parity, offset), table, i, (offset + HALF) * KP, begin, end
+                left, regions, table, i, (offset + HALF) * KP, begin, end
             )
             return carry
 
-        lax.fori_loop(0, blocks, one_row, 0)
-
-    def run(parity, offset):
-        if offset > -HALF:
-            part_unit(parity, offset)
-        else:
-            sign = 1 if parity == 0 else -1
-            whole_unit(parity, sign * HALF)
-            part_unit(parity, -sign * HALF)
+        lax.fori_loop(0, left.shape[0], one_row, 0)
 
     branches(chunk, run)
 
@@ -242,15 +243,22 @@
     )
 
 
-def early_product(chunk, table, left, rights):
-    rights = rights[:4] + rights[5:]
+def whole_product(chunk, table, left, rights):
+    return call(
+        functools.partial(whole_kernel, chunk),
+        [(pltpu.SMEM, table), (pltpu.VMEM, left)] + [flat(rights[k]) for k in (0, 1, 2, 5)],
+        [units_of(left)],
+    )[0]
+
+
+def part_product(chunk, table, left, rights):
     blocks, tile = left.shape[0], left.shape[2]
     partial = jax.ShapeDtypeStruct((blocks, tile, KP * tile), jnp.float32)
     return call(
-        functools.partial(early_kernel, chunk),
-        [(pltpu.SMEM, table), (pltpu.VMEM, left)] + [flat(r) for r in rights],
-        [units_of(left), (pltpu.VMEM, partial)],
-    )
+        functools.partial(part_kernel, chunk),
+        [(pltpu.SMEM, table), (pltpu.VMEM, left)] + [flat(rights[k]) for k in (0, 1, 2, 3, 5)],
+        [(pltpu.VMEM, partial)],
+    )[0]
 
 
 def late_product(chunk, table, left, two, partial):
@@ -329,7 +337,7 @@
     size = blocks * pattern.shape[1] ** 2
     return call(
         functools.partial(table_kernel, blocks=blocks),
-        [(pltpu.SMEM, pattern)],
+        [(pltpu.SMEM, pattern.T)],
         [(pltpu.SMEM, jax.ShapeDtypeStruct((size,), jnp.int32))],
     )[0]
 
@@ -396,7 +404,8 @@
 
     parts = []
     for chunk in range(2):
-        extra, partial = early_product(chunk, table, giant_tiles, babies[chunk])
+        extra = whole_product(chunk, table, giant_tiles, babies[chunk])
+        partial = part_product(chunk, table, giant_tiles, babies[chunk])
         main = late_product(chunk, table, giant_tiles, babies[chunk][4], partial)
         parts += [((chunk, False, True, True), extra), ((chunk, False, False, True), main)]
         main, extra = swapped_parts(chunk, main, extra)

time: 138 us -> 137 us (level)
  waiting for transfers between devices: 65.5 us -> 74.4 us
  local copies, waits for them, and re-layouts: 3.81 us -> 0.02 us
  Pallas kernels: 25.1 us -> 22 us
  starting transfers between devices: 42.1 us -> 39.8 us
    ppermute x24, waiting for transfers between devices: 65.5 us -> 74.4 us  [permute(): return lax.ppermute(block, ('rows', 'rep'), pairs)]
    unnamed x21 -> x8, local copies, waits for them, and re-layouts: 3.81 us -> 0.02 us
    pallas_call x12 -> x14, Pallas kernels: 25.1 us -> 22 us  [call(): pl.pallas_call(kernel, out_shape=[space(out.shape, out.dtype) for space,...]
    ppermute x24, starting transfers between devices: 42.1 us -> 39.8 us  [permute(): return lax.ppermute(block, ('rows', 'rep'), pairs)]
  transfers between devices with their start and end apart: 24 -> 24, of which waited for: 10 -> 11; matrix products, arithmetic and copies ran while one was open for 0% -> 0% of each run, Pallas kernels for 16% -> 14%
where the time goes in v1:
time: 137 us
  waiting for transfers between devices  74.4 us (54%)
  starting transfers between devices  39.8 us (29%)
  Pallas kernels  22 us (16%)
    ppermute x24, waiting for transfers between devices, permute(): return lax.ppermute(block, ('rows', 'rep'), pairs)  74.4 us
    ppermute x24, starting transfers between devices, permute(): return lax.ppermute(block, ('rows', 'rep'), pairs)  39.8 us
    pallas_call x14, Pallas kernels, call(): pl.pallas_call(kernel, out_shape=[space(out.shape, out.dtype) for space,...  22 us
  transfers between devices with their start and end apart: 24, of which 11 were waited for; matrix products, arithmetic and copies ran while one was open for 0% of the time, Pallas kernels for 14%

profile of v1, /device:TPU:1, one launch (start us, length us, event | category | flops | bytes accessed | tf_op | source)
XLA Modules:
  0.0 137.2 jit_solution(10877618450570317630)
XLA Ops:
  0.7 1.4 %shard_map.62 = (bf16[8,2,128,128]{3,2,1,0:T(8,128)(2,1)S(1)}, bf16[8,2,128,128]{3,2,1,0:T(8,128)(2,1)S(1)}) custom-call(bf16[8,10,128,128]{3,2,1,0:T(8,128)(2,1)} %left.9), custom_call_target="tpu_custom_call" | custom-call | flops 1048576 | bytes 8388608 | tf_op jit(solution)/shard_map/pallas_call | solution.py:216
  2.1 2.7 %collective-permute-start.7 = (bf16[8,2,128,128]{3,2,1,0:T(8,128)(2,1)S(1)}, bf16[8,2,128,128]{3,2,1,0:T(8,128)(2,1)S(1)}, u32[]{:S(2)}, u32[]{:S(2)}) collective-permute-start(bf16[8,2,128,128]{3,2,1,0:T(8,128)(2,1)S(1)} %get-tuple-element.19), channel_id=1, source_target_pairs={{0,28},{4,8},{8,4},{12,16},{16,12},{20,24},{24,20},{28,0},{1,29},{... | collective-permute-start | bytes 1572872 | tf_op jit(solution)/shard_map/ppermute | solution.py:39
  6.0 1.3 shard_map.60
  7.3 3.0 %collective-permute-start.1 = (bf16[8,2,128,128]{3,2,1,0:T(8,128)(2,1)S(1)}, bf16[8,2,128,128]{3,2,1,0:T(8,128)(2,1)S(1)}, u32[]{:S(2)}, u32[]{:S(2)}) collective-permute-start(bf16[8,2,128,128]{3,2,1,0:T(8,128)(2,1)S(1)} %get-tuple-element.15), channel_id=1, source_target_pairs={{0,28},{4,8},{8,4},{12,16},{16,12},{20,24},{24,20},{28,0},{1,29},{... | collective-permute-start | bytes 1572872 | tf_op jit(solution)/shard_map/ppermute | solution.py:39
  10.8 5.8 %collective-permute-done.7 = bf16[8,2,128,128]{3,2,1,0:T(8,128)(2,1)S(1)} collective-permute-done((bf16[8,2,128,128]{3,2,1,0:T(8,128)(2,1)S(1)}, bf16[8,2,128,128]{3,2,1,0:T(8,128)(2,1)S(1)}, u32[]{:S(2)}, u32[]{:S(2)}) %collective-permute-start.7) | collective-permute-done | bytes 524320 | tf_op jit(solution)/shard_map/ppermute | solution.py:39
  17.8 11.8 %collective-permute-done.8 = bf16[8,2,128,128]{3,2,1,0:T(8,128)(2,1)S(1)} collective-permute-done((bf16[8,2,128,128]{3,2,1,0:T(8,128)(2,1)S(1)}, bf16[8,2,128,128]{3,2,1,0:T(8,128)(2,1)S(1)}, u32[]{:S(2)}, u32[]{:S(2)}) %collective-permute-start.8) | collective-permute-done | bytes 524320 | tf_op jit(solution)/shard_map/ppermute | solution.py:39
  29.6 1.3 collective-permute-start.2
  31.0 8.1 %collective-permute-done.1 = bf16[8,2,128,128]{3,2,1,0:T(8,128)(2,1)S(1)} collective-permute-done((bf16[8,2,128,128]{3,2,1,0:T(8,128)(2,1)S(1)}, bf16[8,2,128,128]{3,2,1,0:T(8,128)(2,1)S(1)}, u32[]{:S(2)}, u32[]{:S(2)}) %collective-permute-start.1) | collective-permute-done | bytes 524320 | tf_op jit(solution)/shard_map/ppermute | solution.py:39
  39.6 2.9 %shard_map.59.table = s32[800]{0:T(1024)S(4)} custom-call(s32[10,64]{1,0:T(8,128)S(1)} %bitcast.57), custom_call_target="tpu_custom_call" | custom-call | flops 1048576 | bytes 8388608 | tf_op jit(solution)/shard_map/pallas_call | solution.py:216
  42.5 2.8 %shard_map.63 = (bf16[8,2,128,128]{3,2,1,0:T(8,128)(2,1)S(1)}, bf16[8,2,128,128]{3,2,1,0:T(8,128)(2,1)S(1)}, bf16[8,2,128,128]{3,2,1,0:T(8,128)(2,1)S(1)}, bf16[8,2,128,128]{3,2,1,0:T(8,128)(2,1)S(1)}) custom-call(s32[800]{0:T(1024)S(4)} %shard_map.59.table, f32[3]{0:T(128)S(1)} %copy-done.3, bf16[8,10,128,128]{3,2,1,0:T(8,128)(2,1)S(1)} %copy-done.1, ...), custom_call_target="tpu_custom_call" | custom-call | flops 1048576 | bytes 8388608 | tf_op jit(solution)/shard_map/pallas_call | solution.py:216
  46.6 2.8 %shard_map.61 = (bf16[8,2,128,128]{3,2,1,0:T(8,128)(2,1)S(1)}, bf16[8,2,128,128]{3,2,1,0:T(8,128)(2,1)S(1)}, bf16[8,2,128,128]{3,2,1,0:T(8,128)(2,1)S(1)}, bf16[8,2,128,128]{3,2,1,0:T(8,128)(2,1)S(1)}) custom-call(s32[800]{0:T(1024)S(4)} %shard_map.59.table, f32[3]{0:T(128)S(1)} %copy-done.3, bf16[8,10,128,128]{3,2,1,0:T(8,128)(2,1)S(1)} %copy-done.1, ...), custom_call_target="tpu_custom_call" | custom-call | flops 1048576 | bytes 8388608 | tf_op jit(solution)/shard_map/pallas_call | solution.py:216
  49.4 2.4 %collective-permute-start.13 = (bf16[8,2,128,128]{3,2,1,0:T(8,128)(2,1)S(1)}, bf16[8,2,128,128]{3,2,1,0:T(8,128)(2,1)S(1)}, u32[]{:S(2)}, u32[]{:S(2)}) collective-permute-start(bf16[8,2,128,128]{3,2,1,0:T(8,128)(2,1)S(1)} %get-tuple-element.23), channel_id=1, source_target_pairs={{0,28},{4,8},{8,4},{12,16},{16,12},{20,24},{24,20},{28,0},{1,29},{... | collective-permute-start | bytes 1572872 | tf_op jit(solution)/shard_map/ppermute | solution.py:39
  52.7 4.8 %collective-permute-done.19 = bf16[8,2,128,128]{3,2,1,0:T(8,128)(2,1)S(1)} collective-permute-done((bf16[8,2,128,128]{3,2,1,0:T(8,128)(2,1)S(1)}, bf16[8,2,128,128]{3,2,1,0:T(8,128)(2,1)S(1)}, u32[]{:S(2)}, u32[]{:S(2)}) %collective-permute-start.19) | collective-permute-done | bytes 524320 | tf_op jit(solution)/shard_map/ppermute | solution.py:39
  57.6 4.0 %collective-permute-start.20 = (bf16[8,2,128,128]{3,2,1,0:T(8,128)(2,1)S(1)}, bf16[8,2,128,128]{3,2,1,0:T(8,128)(2,1)S(1)}, u32[]{:S(2)}, u32[]{:S(2)}) collective-permute-start(bf16[8,2,128,128]{3,2,1,0:T(8,128)(2,1)S(1)} %collective-permute-done.19), channel_id=1, source_target_pairs={{0,4},{4,0},{8,12},{12,8},{16,20},{20,16},{24,28},{28,24},{1,5},{5... | collective-permute-start | bytes 1572872 | tf_op jit(solution)/shard_map/ppermute | solution.py:39
  61.6 7.2 %collective-permute-done.13 = bf16[8,2,128,128]{3,2,1,0:T(8,128)(2,1)S(1)} collective-permute-done((bf16[8,2,128,128]{3,2,1,0:T(8,128)(2,1)S(1)}, bf16[8,2,128,128]{3,2,1,0:T(8,128)(2,1)S(1)}, u32[]{:S(2)}, u32[]{:S(2)}) %collective-permute-start.13) | collective-permute-done | bytes 524320 | tf_op jit(solution)/shard_map/ppermute | solution.py:39
  68.8 4.0 %collective-permute-start.14 = (bf16[8,2,128,128]{3,2,1,0:T(8,128)(2,1)S(1)}, bf16[8,2,128,128]{3,2,1,0:T(8,128)(2,1)S(1)}, u32[]{:S(2)}, u32[]{:S(2)}) collective-permute-start(bf16[8,2,128,128]{3,2,1,0:T(8,128)(2,1)S(1)} %collective-permute-done.13), channel_id=1, source_target_pairs={{0,4},{4,0},{8,12},{12,8},{16,20},{20,16},{24,28},{28,24},{1,5},{5... | collective-permute-start | bytes 1572872 | tf_op jit(solution)/shard_map/ppermute | solution.py:39
  72.8 1.8 %collective-permute-start.15 = (bf16[8,2,128,128]{3,2,1,0:T(8,128)(2,1)S(1)}, bf16[8,2,128,128]{3,2,1,0:T(8,128)(2,1)S(1)}, u32[]{:S(2)}, u32[]{:S(2)}) collective-permute-start(bf16[8,2,128,128]{3,2,1,0:T(8,128)(2,1)S(1)} %get-tuple-element.22), channel_id=1, source_target_pairs={{0,8},{4,28},{8,16},{16,24},{20,12},{24,0},{1,9},{5,29},{13,5},{17... | collective-permute-start | bytes 1572872 | tf_op jit(solution)/shard_map/ppermute | solution.py:39
  76.0 3.2 %collective-permute-start.10 = (bf16[8,2,128,128]{3,2,1,0:T(8,128)(2,1)S(1)}, bf16[8,2,128,128]{3,2,1,0:T(8,128)(2,1)S(1)}, u32[]{:S(2)}, u32[]{:S(2)}) collective-permute-start(bf16[8,2,128,128]{3,2,1,0:T(8,128)(2,1)S(1)} %get-tuple-element.20.refs_4_), channel_id=1, source_target_pairs={{0,1},{4,5},{8,9},{12,13},{16,17},{20,21},{24,25},{28,29},{1,0},{5... | collective-permute-start | bytes 1572872 | tf_op jit(solution)/shard_map/ppermute | solution.py:39
  80.6 2.2 %collective-permute-start.4 = (bf16[8,2,128,128]{3,2,1,0:T(8,128)(2,1)S(1)}, bf16[8,2,128,128]{3,2,1,0:T(8,128)(2,1)S(1)}, u32[]{:S(2)}, u32[]{:S(2)}) collective-permute-start(bf16[8,2,128,128]{3,2,1,0:T(8,128)(2,1)S(1)} %get-tuple-element.16.refs_0_), channel_id=1, source_target_pairs={{0,1},{4,5},{8,9},{12,13},{16,17},{20,21},{24,25},{28,29},{1,0},{5... | collective-permute-start | bytes 1572872 | tf_op jit(solution)/shard_map/ppermute | solution.py:39
  82.7 1.9 %shard_map.69.partial = f32[8,128,256]{2,1,0:T(8,128)S(1)} custom-call(s32[800]{0:T(1024)S(4)} %shard_map.59.table, bf16[8,10,128,128]{3,2,1,0:T(8,128)(2,1)S(1)} %copy-done, bf16[16,128,128]{2,1,0:T(8,128)(2,1)S(1)} %bitcast.26, bf16[16,128,128]{2,1,0:T(8,128)(2,1)S(1)} %bitcast.28, bf16[16,128,128]{2,1,0:T(8,128)(2,1)S(1)} %bitcast.36, ...), custom_call_target="tpu_custom_call" | custom-call | flops 1048576 | bytes 8388608 | tf_op jit(solution)/shard_map/pallas_call | solution.py:216
  84.7 2.3 %shard_map.66.partial = f32[8,128,256]{2,1,0:T(8,128)S(1)} custom-call(s32[800]{0:T(1024)S(4)} %shard_map.59.table, bf16[8,10,128,128]{3,2,1,0:T(8,128)(2,1)S(1)} %copy-done, bf16[16,128,128]{2,1,0:T(8,128)(2,1)S(1)} %bitcast.30, bf16[16,128,128]{2,1,0:T(8,128)(2,1)S(1)} %bitcast.32, bf16[16,128,128]{2,1,0:T(8,128)(2,1)S(1)} %bitcast.34, ...), custom_call_target="tpu_custom_call" | custom-call | flops 1048576 | bytes 8388608 | tf_op jit(solution)/shard_map/pallas_call | solution.py:216
  87.7 1.4 %shard_map.67.refs_1_ = bf16[8,2,128,128]{3,2,1,0:T(8,128)(2,1)S(1)} custom-call(s32[800]{0:T(1024)S(4)} %shard_map.59.table, bf16[8,10,128,128]{3,2,1,0:T(8,128)(2,1)S(1)} %copy-done, bf16[16,128,128]{2,1,0:T(8,128)(2,1)S(1)} %bitcast.52, f32[8,128,256]{2,1,0:T(8,128)S(1)} %shard_map.66.partial), custom_call_target="tpu_custom_call" | custom-call | flops 1048576 | bytes 8388608 | tf_op jit(solution)/shard_map/pallas_call | solution.py:216
  89.1 1.4 %collective-permute-done.21 = bf16[8,2,128,128]{3,2,1,0:T(8,128)(2,1)S(1)} collective-permute-done((bf16[8,2,128,128]{3,2,1,0:T(8,128)(2,1)S(1)}, bf16[8,2,128,128]{3,2,1,0:T(8,128)(2,1)S(1)}, u32[]{:S(2)}, u32[]{:S(2)}) %collective-permute-start.21) | collective-permute-done | bytes 524320 | tf_op jit(solution)/shard_map/ppermute | solution.py:39
  91.8 4.2 %collective-permute-start.17 = (bf16[8,2,128,128]{3,2,1,0:T(8,128)(2,1)S(1)}, bf16[8,2,128,128]{3,2,1,0:T(8,128)(2,1)S(1)}, u32[]{:S(2)}, u32[]{:S(2)}) collective-permute-start(bf16[8,2,128,128]{3,2,1,0:T(8,128)(2,1)S(1)} %shard_map.67.refs_1_), channel_id=1, source_target_pairs={{0,1},{4,5},{8,9},{12,13},{16,17},{20,21},{24,25},{28,29},{1,0},{5... | collective-permute-start | bytes 1572872 | tf_op jit(solution)/shard_map/ppermute | solution.py:39
  96.1 5.0 %collective-permute-done.11.refs_7_ = bf16[8,2,128,128]{3,2,1,0:T(8,128)(2,1)S(1)} collective-permute-done((bf16[8,2,128,128]{3,2,1,0:T(8,128)(2,1)S(1)}, bf16[8,2,128,128]{3,2,1,0:T(8,128)(2,1)S(1)}, u32[]{:S(2)}, u32[]{:S(2)}) %collective-permute-start.11) | collective-permute-done | bytes 524320 | tf_op jit(solution)/shard_map/ppermute | solution.py:39
  101.7 1.4 %shard_map.70.refs_5_ = bf16[8,2,128,128]{3,2,1,0:T(8,128)(2,1)S(1)} custom-call(s32[800]{0:T(1024)S(4)} %shard_map.59.table, bf16[8,10,128,128]{3,2,1,0:T(8,128)(2,1)S(1)} %copy-done, bf16[16,128,128]{2,1,0:T(8,128)(2,1)S(1)} %bitcast.44, f32[8,128,256]{2,1,0:T(8,128)S(1)} %shard_map.69.partial), custom_call_target="tpu_custom_call" | custom-call | flops 1048576 | bytes 8388608 | tf_op jit(solution)/shard_map/pallas_call | solution.py:216
  103.2 9.1 %collective-permute-done.4.refs_2_ = bf16[8,2,128,128]{3,2,1,0:T(8,128)(2,1)S(1)} collective-permute-done((bf16[8,2,128,128]{3,2,1,0:T(8,128)(2,1)S(1)}, bf16[8,2,128,128]{3,2,1,0:T(8,128)(2,1)S(1)}, u32[]{:S(2)}, u32[]{:S(2)}) %collective-permute-start.4) | collective-permute-done | bytes 524320 | tf_op jit(solution)/shard_map/ppermute | solution.py:39
  112.3 1.6 %shard_map.64 = bf16[8,10,128,128]{3,2,1,0:T(8,128)(2,1)} custom-call(bf16[8,2,128,128]{3,2,1,0:T(8,128)(2,1)S(1)} %get-tuple-element.16.refs_0_, bf16[8,2,128,128]{3,2,1,0:T(8,128)(2,1)S(1)} %get-tuple-element.17.refs_1_, bf16[8,2,128,128]{3,2,1,0:T(8,128)(2,1)S(1)} %collective-permute-done.4.refs_2_, ...), custom_call_target="tpu_custom_call" | custom-call | flops 1048576 | bytes 8388608 | tf_op jit(solution)/shard_map/pallas_call | solution.py:216
  113.8 8.1 %collective-permute-done.22.refs_6_ = bf16[8,2,128,128]{3,2,1,0:T(8,128)(2,1)S(1)} collective-permute-done((bf16[8,2,128,128]{3,2,1,0:T(8,128)(2,1)S(1)}, bf16[8,2,128,128]{3,2,1,0:T(8,128)(2,1)S(1)}, u32[]{:S(2)}, u32[]{:S(2)}) %collective-permute-start.22) | collective-permute-done | bytes 524320 | tf_op jit(solution)/shard_map/ppermute | solution.py:39
  122.0 8.8 %collective-permute-done.17.refs_3_ = bf16[8,2,128,128]{3,2,1,0:T(8,128)(2,1)S(1)} collective-permute-done((bf16[8,2,128,128]{3,2,1,0:T(8,128)(2,1)S(1)}, bf16[8,2,128,128]{3,2,1,0:T(8,128)(2,1)S(1)}, u32[]{:S(2)}, u32[]{:S(2)}) %collective-permute-start.17) | collective-permute-done | bytes 524320 | tf_op jit(solution)/shard_map/ppermute | solution.py:39
  130.8 1.4 shard_map.71.refs_0_
  132.1 4.2 %collective-permute-done.23.refs_1_ = bf16[8,2,128,128]{3,2,1,0:T(8,128)(2,1)S(1)} collective-permute-done((bf16[8,2,128,128]{3,2,1,0:T(8,128)(2,1)S(1)}, bf16[8,2,128,128]{3,2,1,0:T(8,128)(2,1)S(1)}, u32[]{:S(2)}, u32[]{:S(2)}) %collective-permute-start.23) | collective-permute-done | bytes 524320 | tf_op jit(solution)/shard_map/ppermute | solution.py:39
  (38 shorter events, 11.8 us)
Async XLA Ops:
  0.6 41.9 %copy-start.1 = (bf16[8,10,128,128]{3,2,1,0:T(8,128)(2,1)S(1)}, bf16[8,10,128,128]{3,2,1,0:T(8,128)(2,1)}, u32[]{:S(2)}) copy-start(bf16[8,10,128,128]{3,2,1,0:T(8,128)(2,1)} %left.9) | copy-start | bytes 7864324
  0.6 39.0 %copy-start.2 = (s32[64,10]{0,1:T(8,128)S(1)}, s32[64,10]{0,1:T(8,128)}, u32[]{:S(2)}) copy-start(s32[64,10]{0,1:T(8,128)} %param.7) | copy-start | bytes 7684
  0.7 41.9 %copy-start.3 = (f32[3]{0:T(128)S(1)}, f32[3]{0:T(128)}, u32[]{:S(2)}) copy-start(f32[3]{0:T(128)} %coeffs.3) | copy-start | bytes 40
  2.1 14.5 %collective-permute-start.7 = (bf16[8,2,128,128]{3,2,1,0:T(8,128)(2,1)S(1)}, bf16[8,2,128,128]{3,2,1,0:T(8,128)(2,1)S(1)}, u32[]{:S(2)}, u32[]{:S(2)}) collective-permute-start(bf16[8,2,128,128]{3,2,1,0:T(8,128)(2,1)S(1)} %get-tuple-element.19), channel_id=1, source_target_pairs={{0,28},{4,8},{8,4},{12,16},{16,12},{20,24},{24,20},{28,0},{1,29},{... | collective-permute-start | bytes 1572872 | tf_op jit(solution)/shard_map/ppermute | solution.py:39
  4.7 24.9 %collective-permute-start.8 = (bf16[8,2,128,128]{3,2,1,0:T(8,128)(2,1)S(1)}, bf16[8,2,128,128]{3,2,1,0:T(8,128)(2,1)S(1)}, u32[]{:S(2)}, u32[]{:S(2)}) collective-permute-start(bf16[8,2,128,128]{3,2,1,0:T(8,128)(2,1)S(1)} %get-tuple-element.18), channel_id=1, source_target_pairs={{0,8},{8,16},{12,4},{16,24},{24,0},{28,20},{5,29},{9,17},{13,5},{2... | collective-permute-start | bytes 1572872 | tf_op jit(solution)/shard_map/ppermute | solution.py:39
  7.3 31.7 %collective-permute-start.1 = (bf16[8,2,128,128]{3,2,1,0:T(8,128)(2,1)S(1)}, bf16[8,2,128,128]{3,2,1,0:T(8,128)(2,1)S(1)}, u32[]{:S(2)}, u32[]{:S(2)}) collective-permute-start(bf16[8,2,128,128]{3,2,1,0:T(8,128)(2,1)S(1)} %get-tuple-element.15), channel_id=1, source_target_pairs={{0,28},{4,8},{8,4},{12,16},{16,12},{20,24},{24,20},{28,0},{1,29},{... | collective-permute-start | bytes 1572872 | tf_op jit(solution)/shard_map/ppermute | solution.py:39
  10.3 32.2 %collective-permute-start.6 = (bf16[8,2,128,128]{3,2,1,0:T(8,128)(2,1)S(1)}, bf16[8,2,128,128]{3,2,1,0:T(8,128)(2,1)S(1)}, u32[]{:S(2)}, u32[]{:S(2)}) collective-permute-start(bf16[8,2,128,128]{3,2,1,0:T(8,128)(2,1)S(1)} %get-tuple-element.18), channel_id=1, source_target_pairs={{0,4},{4,0},{8,12},{12,8},{16,20},{20,16},{24,28},{28,24},{1,5},{5... | collective-permute-start | bytes 1572872 | tf_op jit(solution)/shard_map/ppermute | solution.py:39
  16.6 25.9 %collective-permute-start.9 = (bf16[8,2,128,128]{3,2,1,0:T(8,128)(2,1)S(1)}, bf16[8,2,128,128]{3,2,1,0:T(8,128)(2,1)S(1)}, u32[]{:S(2)}, u32[]{:S(2)}) collective-permute-start(bf16[8,2,128,128]{3,2,1,0:T(8,128)(2,1)S(1)} %collective-permute-done.7), channel_id=1, source_target_pairs={{0,4},{4,0},{8,12},{12,8},{16,20},{20,16},{24,28},{28,24},{1,5},{5... | collective-permute-start | bytes 1572872 | tf_op jit(solution)/shard_map/ppermute | solution.py:39
  17.8 28.8 %collective-permute-start = (bf16[8,2,128,128]{3,2,1,0:T(8,128)(2,1)S(1)}, bf16[8,2,128,128]{3,2,1,0:T(8,128)(2,1)S(1)}, u32[]{:S(2)}, u32[]{:S(2)}) collective-permute-start(bf16[8,2,128,128]{3,2,1,0:T(8,128)(2,1)S(1)} %get-tuple-element.14), channel_id=1, source_target_pairs={{0,4},{4,0},{8,12},{12,8},{16,20},{20,16},{24,28},{28,24},{1,5},{5... | collective-permute-start | bytes 1572872 | tf_op jit(solution)/shard_map/ppermute | solution.py:39
  29.6 16.9 %collective-permute-start.2 = (bf16[8,2,128,128]{3,2,1,0:T(8,128)(2,1)S(1)}, bf16[8,2,128,128]{3,2,1,0:T(8,128)(2,1)S(1)}, u32[]{:S(2)}, u32[]{:S(2)}) collective-permute-start(bf16[8,2,128,128]{3,2,1,0:T(8,128)(2,1)S(1)} %get-tuple-element.14), channel_id=1, source_target_pairs={{0,8},{4,28},{8,16},{16,24},{20,12},{24,0},{1,9},{5,29},{13,5},{17... | collective-permute-start | bytes 1572872 | tf_op jit(solution)/shard_map/ppermute | solution.py:39
  39.1 7.5 %collective-permute-start.3 = (bf16[8,2,128,128]{3,2,1,0:T(8,128)(2,1)S(1)}, bf16[8,2,128,128]{3,2,1,0:T(8,128)(2,1)S(1)}, u32[]{:S(2)}, u32[]{:S(2)}) collective-permute-start(bf16[8,2,128,128]{3,2,1,0:T(8,128)(2,1)S(1)} %collective-permute-done.1), channel_id=1, source_target_pairs={{0,4},{4,0},{8,12},{12,8},{16,20},{20,16},{24,28},{28,24},{1,5},{5... | collective-permute-start | bytes 1572872 | tf_op jit(solution)/shard_map/ppermute | solution.py:39
  45.4 12.2 %collective-permute-start.19 = (bf16[8,2,128,128]{3,2,1,0:T(8,128)(2,1)S(1)}, bf16[8,2,128,128]{3,2,1,0:T(8,128)(2,1)S(1)}, u32[]{:S(2)}, u32[]{:S(2)}) collective-permute-start(bf16[8,2,128,128]{3,2,1,0:T(8,128)(2,1)S(1)} %get-tuple-element.25), channel_id=1, source_target_pairs={{0,28},{4,8},{8,4},{12,16},{16,12},{20,24},{24,20},{28,0},{1,29},{... | collective-permute-start | bytes 1572872 | tf_op jit(solution)/shard_map/ppermute | solution.py:39
  46.6 36.1 %copy-start = (bf16[8,10,128,128]{3,2,1,0:T(8,128)(2,1)S(1)}, bf16[8,10,128,128]{3,2,1,0:T(8,128)(2,1)}, u32[]{:S(2)}) copy-start(bf16[8,10,128,128]{3,2,1,0:T(8,128)(2,1)} %left.15) | copy-start | bytes 7864324
  49.4 19.4 %collective-permute-start.13 = (bf16[8,2,128,128]{3,2,1,0:T(8,128)(2,1)S(1)}, bf16[8,2,128,128]{3,2,1,0:T(8,128)(2,1)S(1)}, u32[]{:S(2)}, u32[]{:S(2)}) collective-permute-start(bf16[8,2,128,128]{3,2,1,0:T(8,128)(2,1)S(1)} %get-tuple-element.23), channel_id=1, source_target_pairs={{0,28},{4,8},{8,4},{12,16},{16,12},{20,24},{24,20},{28,0},{1,29},{... | collective-permute-start | bytes 1572872 | tf_op jit(solution)/shard_map/ppermute | solution.py:39
  51.8 22.9 %collective-permute-start.18 = (bf16[8,2,128,128]{3,2,1,0:T(8,128)(2,1)S(1)}, bf16[8,2,128,128]{3,2,1,0:T(8,128)(2,1)S(1)}, u32[]{:S(2)}, u32[]{:S(2)}) collective-permute-start(bf16[8,2,128,128]{3,2,1,0:T(8,128)(2,1)S(1)} %get-tuple-element.24), channel_id=1, source_target_pairs={{0,4},{4,0},{8,12},{12,8},{16,20},{20,16},{24,28},{28,24},{1,5},{5... | collective-permute-start | bytes 1572872 | tf_op jit(solution)/shard_map/ppermute | solution.py:39
  52.7 23.3 %collective-permute-start.12 = (bf16[8,2,128,128]{3,2,1,0:T(8,128)(2,1)S(1)}, bf16[8,2,128,128]{3,2,1,0:T(8,128)(2,1)S(1)}, u32[]{:S(2)}, u32[]{:S(2)}) collective-permute-start(bf16[8,2,128,128]{3,2,1,0:T(8,128)(2,1)S(1)} %get-tuple-element.22), channel_id=1, source_target_pairs={{0,4},{4,0},{8,12},{12,8},{16,20},{20,16},{24,28},{28,24},{1,5},{5... | collective-permute-start | bytes 1572872 | tf_op jit(solution)/shard_map/ppermute | solution.py:39
  57.6 21.7 %collective-permute-start.20 = (bf16[8,2,128,128]{3,2,1,0:T(8,128)(2,1)S(1)}, bf16[8,2,128,128]{3,2,1,0:T(8,128)(2,1)S(1)}, u32[]{:S(2)}, u32[]{:S(2)}) collective-permute-start(bf16[8,2,128,128]{3,2,1,0:T(8,128)(2,1)S(1)} %collective-permute-done.19), channel_id=1, source_target_pairs={{0,4},{4,0},{8,12},{12,8},{16,20},{20,16},{24,28},{28,24},{1,5},{5... | collective-permute-start | bytes 1572872 | tf_op jit(solution)/shard_map/ppermute | solution.py:39
  68.8 11.8 %collective-permute-start.14 = (bf16[8,2,128,128]{3,2,1,0:T(8,128)(2,1)S(1)}, bf16[8,2,128,128]{3,2,1,0:T(8,128)(2,1)S(1)}, u32[]{:S(2)}, u32[]{:S(2)}) collective-permute-start(bf16[8,2,128,128]{3,2,1,0:T(8,128)(2,1)S(1)} %collective-permute-done.13), channel_id=1, source_target_pairs={{0,4},{4,0},{8,12},{12,8},{16,20},{20,16},{24,28},{28,24},{1,5},{5... | collective-permute-start | bytes 1572872 | tf_op jit(solution)/shard_map/ppermute | solution.py:39
  72.8 14.1 %collective-permute-start.15 = (bf16[8,2,128,128]{3,2,1,0:T(8,128)(2,1)S(1)}, bf16[8,2,128,128]{3,2,1,0:T(8,128)(2,1)S(1)}, u32[]{:S(2)}, u32[]{:S(2)}) collective-permute-start(bf16[8,2,128,128]{3,2,1,0:T(8,128)(2,1)S(1)} %get-tuple-element.22), channel_id=1, source_target_pairs={{0,8},{4,28},{8,16},{16,24},{20,12},{24,0},{1,9},{5,29},{13,5},{17... | collective-permute-start | bytes 1572872 | tf_op jit(solution)/shard_map/ppermute | solution.py:39
  74.7 15.8 %collective-permute-start.21 = (bf16[8,2,128,128]{3,2,1,0:T(8,128)(2,1)S(1)}, bf16[8,2,128,128]{3,2,1,0:T(8,128)(2,1)S(1)}, u32[]{:S(2)}, u32[]{:S(2)}) collective-permute-start(bf16[8,2,128,128]{3,2,1,0:T(8,128)(2,1)S(1)} %get-tuple-element.24), channel_id=1, source_target_pairs={{0,8},{8,16},{12,4},{16,24},{24,0},{28,20},{5,29},{9,17},{13,5},{2... | collective-permute-start | bytes 1572872 | tf_op jit(solution)/shard_map/ppermute | solution.py:39
  76.0 15.8 %collective-permute-start.10 = (bf16[8,2,128,128]{3,2,1,0:T(8,128)(2,1)S(1)}, bf16[8,2,128,128]{3,2,1,0:T(8,128)(2,1)S(1)}, u32[]{:S(2)}, u32[]{:S(2)}) collective-permute-start(bf16[8,2,128,128]{3,2,1,0:T(8,128)(2,1)S(1)} %get-tuple-element.20.refs_4_), channel_id=1, source_target_pairs={{0,1},{4,5},{8,9},{12,13},{16,17},{20,21},{24,25},{28,29},{1,0},{5... | collective-permute-start | bytes 1572872 | tf_op jit(solution)/shard_map/ppermute | solution.py:39
  79.3 21.8 %collective-permute-start.11 = (bf16[8,2,128,128]{3,2,1,0:T(8,128)(2,1)S(1)}, bf16[8,2,128,128]{3,2,1,0:T(8,128)(2,1)S(1)}, u32[]{:S(2)}, u32[]{:S(2)}) collective-permute-start(bf16[8,2,128,128]{3,2,1,0:T(8,128)(2,1)S(1)} %get-tuple-element.21.refs_5_), channel_id=1, source_target_pairs={{0,1},{16,17},{5,4},{21,20},{2,3},{18,19},{7,6},{23,22}} | collective-permute-start | bytes 1572872 | tf_op jit(solution)/shard_map/ppermute | solution.py:39
  80.6 31.7 %collective-permute-start.4 = (bf16[8,2,128,128]{3,2,1,0:T(8,128)(2,1)S(1)}, bf16[8,2,128,128]{3,2,1,0:T(8,128)(2,1)S(1)}, u32[]{:S(2)}, u32[]{:S(2)}) collective-permute-start(bf16[8,2,128,128]{3,2,1,0:T(8,128)(2,1)S(1)} %get-tuple-element.16.refs_0_), channel_id=1, source_target_pairs={{0,1},{4,5},{8,9},{12,13},{16,17},{20,21},{24,25},{28,29},{1,0},{5... | collective-permute-start | bytes 1572872 | tf_op jit(solution)/shard_map/ppermute | solution.py:39
  87.0 25.3 %collective-permute-start.5 = (bf16[8,2,128,128]{3,2,1,0:T(8,128)(2,1)S(1)}, bf16[8,2,128,128]{3,2,1,0:T(8,128)(2,1)S(1)}, u32[]{:S(2)}, u32[]{:S(2)}) collective-permute-start(bf16[8,2,128,128]{3,2,1,0:T(8,128)(2,1)S(1)} %get-tuple-element.17.refs_1_), channel_id=1, source_target_pairs={{8,9},{24,25},{13,12},{29,28},{10,11},{26,27},{15,14},{31,30}} | collective-permute-start | bytes 1572872 | tf_op jit(solution)/shard_map/ppermute | solution.py:39
  90.5 31.4 %collective-permute-start.22 = (bf16[8,2,128,128]{3,2,1,0:T(8,128)(2,1)S(1)}, bf16[8,2,128,128]{3,2,1,0:T(8,128)(2,1)S(1)}, u32[]{:S(2)}, u32[]{:S(2)}) collective-permute-start(bf16[8,2,128,128]{3,2,1,0:T(8,128)(2,1)S(1)} %shard_map.68.refs_4_), channel_id=1, source_target_pairs={{0,1},{16,17},{5,4},{21,20},{2,3},{18,19},{7,6},{23,22}} | collective-permute-start | bytes 1572872 | tf_op jit(solution)/shard_map/ppermute | solution.py:39
  91.8 38.9 %collective-permute-start.17 = (bf16[8,2,128,128]{3,2,1,0:T(8,128)(2,1)S(1)}, bf16[8,2,128,128]{3,2,1,0:T(8,128)(2,1)S(1)}, u32[]{:S(2)}, u32[]{:S(2)}) collective-permute-start(bf16[8,2,128,128]{3,2,1,0:T(8,128)(2,1)S(1)} %shard_map.67.refs_1_), channel_id=1, source_target_pairs={{0,1},{4,5},{8,9},{12,13},{16,17},{20,21},{24,25},{28,29},{1,0},{5... | collective-permute-start | bytes 1572872 | tf_op jit(solution)/shard_map/ppermute | solution.py:39
  101.0 29.7 %collective-permute-start.16 = (bf16[8,2,128,128]{3,2,1,0:T(8,128)(2,1)S(1)}, bf16[8,2,128,128]{3,2,1,0:T(8,128)(2,1)S(1)}, u32[]{:S(2)}, u32[]{:S(2)}) collective-permute-start(bf16[8,2,128,128]{3,2,1,0:T(8,128)(2,1)S(1)} %shard_map.65.refs_0_), channel_id=1, source_target_pairs={{8,9},{24,25},{13,12},{29,28},{10,11},{26,27},{15,14},{31,30}} | collective-permute-start | bytes 1572872 | tf_op jit(solution)/shard_map/ppermute | solution.py:39
  112.3 24.1 %collective-permute-start.23 = (bf16[8,2,128,128]{3,2,1,0:T(8,128)(2,1)S(1)}, bf16[8,2,128,128]{3,2,1,0:T(8,128)(2,1)S(1)}, u32[]{:S(2)}, u32[]{:S(2)}) collective-permute-start(bf16[8,2,128,128]{3,2,1,0:T(8,128)(2,1)S(1)} %shard_map.70.refs_5_), channel_id=1, source_target_pairs={{0,1},{4,5},{8,9},{12,13},{16,17},{20,21},{24,25},{28,29},{1,0},{5... | collective-permute-start | bytes 1572872 | tf_op jit(solution)/shard_map/ppermute | solution.py:39
